TPU v7x, 128 devices: a whole 4x4x4 slice. The times are simulated.
128 devices in a mesh: pool: 128 (over z, y, x, core).
Axes of the slice: x: 4, y: 4, z: 4, core: 2. Of those that a mesh axis runs over, the one named last changes fastest.
Arguments:
- queries: bfloat16 [128, 128, 64, 128], P('pool')
- k_new: bfloat16 [128, 128, 8, 128], P('pool')
- v_new: bfloat16 [128, 128, 8, 128], P('pool')
- k_pool: bfloat16 [4096, 16, 8, 128], P('pool')
- v_pool: bfloat16 [4096, 16, 8, 128], P('pool')
- block_table: int32 [128, 64], replicated
- write_ids: int32 [128, 8], P('pool')
Outputs:
- output 1: bfloat16 [128, 128, 64, 128], P('pool')
- output 2: bfloat16 [4096, 16, 8, 128], P('pool')
- output 3: bfloat16 [4096, 16, 8, 128], P('pool')
All inputs are finite; a program needn't handle non-finite values.
Results may differ from a plain program's by a relative error of at most 0.00941793.
Values are sent between devices in bfloat16 or wider.
A program may use at most 1 GiB of HBM per device.

v0:
```python
import jax
import jax.numpy as jnp
from jax import lax
from jax.sharding import PartitionSpec as P


def chunk_attention(q_grp, k_pref, v_pref, k_chunk, v_chunk):
    chunk_len = q_grp.shape[1]
    score_scale = q_grp.shape[-1] ** -0.5
    s_pref = jnp.einsum('rcgqd,rtgd->rcgqt', q_grp, k_pref, preferred_element_type=jnp.float32) * score_scale
    s_self = jnp.einsum('rcgqd,rtgd->rcgqt', q_grp, k_chunk, preferred_element_type=jnp.float32) * score_scale
    causal = (jnp.arange(chunk_len)[:, None] >= jnp.arange(chunk_len)[None, :])[None, :, None, None, :]
    s_self = jnp.where(causal, s_self, -jnp.inf)
    row_max = jnp.maximum(jnp.max(s_pref, axis=-1), jnp.max(s_self, axis=-1))[..., None]
    e_pref = jnp.exp(s_pref - row_max)
    e_self = jnp.exp(s_self - row_max)
    prob_total = jnp.sum(e_pref, axis=-1, keepdims=True) + jnp.sum(e_self, axis=-1, keepdims=True)
    p_pref = (e_pref / prob_total).astype(jnp.bfloat16)
    p_self = (e_self / prob_total).astype(jnp.bfloat16)
    attn_acc = jnp.einsum('rcgqt,rtgd->rcgqd', p_pref, v_pref, preferred_element_type=jnp.float32)
    return attn_acc + jnp.einsum('rcgqt,rtgd->rcgqd', p_self, v_chunk, preferred_element_type=jnp.float32)


def solution(mesh):
    n_dev = mesh.shape['pool']

    def local_step(queries, k_new, v_new, k_pool, v_pool, block_table, write_ids):
        req_count, chunk_len, q_heads, head_dim = queries.shape
        kv_heads = k_new.shape[2]
        per_dev, block_len = k_pool.shape[0], k_pool.shape[1]
        n_pref = block_table.shape[1]
        row_cap = 2 * n_pref // n_dev + (n_pref // 2 + n_dev - 1) // n_dev
        pair_cap = req_count * row_cap
        my_index = lax.axis_index('pool')
        owners = block_table // per_dev
        owned_here = (owners == my_index).reshape(n_dev, req_count * n_pref).astype(jnp.int32)
        send_slot = jnp.where(owned_here > 0, jnp.cumsum(owned_here, axis=1) - 1, pair_cap)
        dest_dev = jnp.broadcast_to(jnp.arange(n_dev)[:, None], send_slot.shape)
        local_ids = (block_table % per_dev).reshape(n_dev, req_count * n_pref)
        send_ids = jnp.zeros((n_dev, pair_cap), jnp.int32).at[dest_dev, send_slot].set(local_ids, mode='drop')
        k_recv = lax.all_to_all(k_pool[send_ids], 'pool', 0, 0, tiled=True)
        v_recv = lax.all_to_all(v_pool[send_ids], 'pool', 0, 0, tiled=True)
        my_owners = lax.dynamic_slice_in_dim(owners, my_index * req_count, req_count, 0).reshape(-1)
        from_owner = (my_owners[:, None] == jnp.arange(n_dev)[None, :]).astype(jnp.int32)
        slot_rank = jnp.sum(from_owner * (jnp.cumsum(from_owner, axis=0) - 1), axis=1)
        recv_idx = (my_owners * pair_cap + slot_rank).reshape(req_count, n_pref)
        flat_shape = (n_dev * pair_cap, block_len, kv_heads, head_dim)
        prefix_shape = (req_count, n_pref * block_len, kv_heads, head_dim)
        k_pref = k_recv.reshape(flat_shape)[recv_idx].reshape(prefix_shape)
        v_pref = v_recv.reshape(flat_shape)[recv_idx].reshape(prefix_shape)
        q_grp = queries.reshape(req_count, chunk_len, kv_heads, q_heads // kv_heads, head_dim)
        attn_acc = chunk_attention(q_grp, k_pref, v_pref, k_new, v_new)
        attn_out = attn_acc.reshape(req_count, chunk_len, q_heads, head_dim).astype(jnp.bfloat16)
        new_shape = (req_count * chunk_len // block_len, block_len, kv_heads, head_dim)
        targets = write_ids.reshape(-1)
        k_pool_out = k_pool.at[targets].set(k_new.reshape(new_shape))
        v_pool_out = v_pool.at[targets].set(v_new.reshape(new_shape))
        return attn_out, k_pool_out, v_pool_out

    row_spec = P('pool')
    return jax.shard_map(local_step, mesh=mesh, in_specs=(row_spec, row_spec, row_spec, row_spec, row_spec, P(), row_spec), out_specs=(row_spec, row_spec, row_spec), check_vma=False)
```

profile of v0, /device:TPU:1, one launch (start us, length us, event | category | flops | bytes accessed | tf_op | source)
XLA Modules:
  0.0 352.9 jit_solution(13401954734374692146)
XLA Ops:
  0.7 2.5 copy.86
  3.1 1.2 copy.85
  4.4 0.1 copy.33
  4.6 0.1 reduce_window_sum.22
  4.7 0.1 and_reduce_fusion
  4.8 0.1 multiply_reduce_fusion
  4.9 0.1 copy.32
  5.1 30.4 %scatter_custom_fusion.2 = s32[256]{0:T(256)S(1)} fusion(s32[8192]{0:T(1024)S(1)} %reshape.233, s32[8192]{0:T(1024)S(1)} %reshape.235, s32[]{:T(128)} %constant.28.clone.1), kind=kCustom, calls=%fused_computation.62 | custom fusion | bytes 1028
  35.5 0.1 copy.34
  35.6 0.1 reshape.187
  35.8 9.6 %gather_fusion = bf16[256,16,8,128]{3,2,1,0:T(8,128)(2,1)} fusion(bf16[32,16,8,128]{3,2,1,0:T(8,128)(2,1)} %copy.86, s32[1024]{0:T(1024)S(1)} %pad_clamp_fusion.1), kind=kCustom, calls=%fused_computation | custom fusion | bytes 16778240 | tf_op jit(solution)/shard_map/gather | solution.py:42
  45.4 12.0 %all-to-all-start = ((bf16[128,2,16,8,128]{4,3,2,1,0:T(8,128)(2,1)}), bf16[128,2,16,8,128]{4,3,2,1,0:T(8,128)(2,1)}, u32[]{:S(2)}, u32[]{:S(2)}) async-start(bf16[128,2,16,8,128]{4,3,2,1,0:T(8,128)(2,1)} %bitcast.78), calls=%async_computation | async-start | bytes 16777216 | tf_op jit(solution)/shard_map/all_to_all | solution.py:42
  57.4 8.4 %gather_fusion.2 = bf16[256,16,8,128]{3,2,1,0:T(8,128)(2,1)} fusion(bf16[32,16,8,128]{3,2,1,0:T(8,128)(2,1)S(1)} %copy.85, s32[1024]{0:T(1024)S(1)} %pad_clamp_fusion.1), kind=kCustom, calls=%fused_computation.2 | custom fusion | bytes 16778240 | tf_op jit(solution)/shard_map/gather | solution.py:41
  65.8 104.5 %all-to-all-done = bf16[128,2,16,8,128]{4,3,2,1,0:T(8,128)(2,1)} async-done(((bf16[128,2,16,8,128]{4,3,2,1,0:T(8,128)(2,1)}), bf16[128,2,16,8,128]{4,3,2,1,0:T(8,128)(2,1)}, u32[]{:S(2)}, u32[]{:S(2)}) %all-to-all-start) | async-done | bytes 8388640 | tf_op jit(solution)/shard_map/all_to_all | solution.py:42
  170.3 11.4 %all-to-all-start.1 = ((bf16[128,2,16,8,128]{4,3,2,1,0:T(8,128)(2,1)}), bf16[128,2,16,8,128]{4,3,2,1,0:T(8,128)(2,1)}, u32[]{:S(2)}, u32[]{:S(2)}) async-start(bf16[128,2,16,8,128]{4,3,2,1,0:T(8,128)(2,1)} %bitcast.77), calls=%async_computation.1 | async-start | bytes 16777216 | tf_op jit(solution)/shard_map/all_to_all | solution.py:41
  181.7 0.2 dynamic-slice_reduce_fusion
  182.0 0.1 reduce_window_sum.23
  182.1 0.2 select_reduce_fusion
  182.2 0.1 copy.35
  182.4 2.4 scatter_fusion.1
  184.8 0.8 scatter_fusion
  185.6 0.2 fusion.22
  185.8 4.0 %fusion.7 = (f32[128,8,8]{0,2,1:T(8,128)S(1)}, f32[8,128,128,8]{2,1,3,0:T(8,128)}) fusion(pred[128,128]{0,1:T(8,128)(4,1)S(1)} %iota_compare_fusion, bf16[128,8,8,128]{3,2,1,0:T(8,128)(2,1)S(1)} %bitcast.76, bf16[128,8,128,1]{2,1,0,3:T(8,128)(2,1)S(1)} %bitcast.83), kind=kOutput, calls=%fused_computation.21 | convolution fusion | flops 271572992 | bytes 6602752 | tf_op jit(solution)/shard_map/rcgqd,rtgd->rcgqt/dot_general | solution.py:11
  189.8 5.5 %gather_fusion.1 = bf16[64,16,8,128]{3,2,1,0:T(8,128)(2,1)} fusion(bf16[256,16,8,128]{3,2,1,0:T(8,128)(2,1)} %bitcast.5, s32[1024]{0:T(1024)S(1)} %pad_clamp_fusion), kind=kCustom, calls=%fused_computation.1 | custom fusion | bytes 4194560 | tf_op jit(solution)/shard_map/gather | solution.py:50
  195.3 95.4 %all-to-all-done.1 = bf16[128,2,16,8,128]{4,3,2,1,0:T(8,128)(2,1)} async-done(((bf16[128,2,16,8,128]{4,3,2,1,0:T(8,128)(2,1)}), bf16[128,2,16,8,128]{4,3,2,1,0:T(8,128)(2,1)}, u32[]{:S(2)}, u32[]{:S(2)}) %all-to-all-start.1) | async-done | bytes 8388640 | tf_op jit(solution)/shard_map/all_to_all | solution.py:41
  290.7 5.5 %gather_fusion.3 = bf16[64,16,8,128]{3,2,1,0:T(8,128)(2,1)} fusion(bf16[256,16,8,128]{3,2,1,0:T(8,128)(2,1)} %bitcast.10, s32[1024]{0:T(1024)S(1)} %pad_clamp_fusion), kind=kCustom, calls=%fused_computation.3 | custom fusion | bytes 4194560 | tf_op jit(solution)/shard_map/gather | solution.py:49
  296.2 15.7 %bitcast_reduce_fusion = (f32[128,8,8]{0,2,1:T(8,128)S(1)}, f32[8,1024,128,8]{2,1,3,0:T(8,128)}) fusion(bf16[128,8,8,128]{3,2,1,0:T(8,128)(2,1)S(1)} %bitcast.75, bf16[1024,8,128,1]{2,1,0,3:T(8,128)(2,1)} %bitcast.79), kind=kOutput, calls=%fused_computation.8 | convolution fusion | flops 2164252672 | bytes 37781504 | tf_op jit(solution)/shard_map/rcgqd,rtgd->rcgqt/dot_general | solution.py:10
  311.9 1.1 fusion.6
  313.0 13.7 %fusion.1 = f32[128,8,8]{0,2,1:T(8,128)S(1)} fusion(f32[8,1024,128,8]{2,1,3,0:T(8,128)} %get-tuple-element.15, f32[128,8,8]{0,2,1:T(8,128)S(1)} %max.9), kind=kLoop, calls=%fused_computation.11 | loop fusion | flops 25157632 | bytes 33619968 | tf_op jit(solution)/shard_map/reduce_sum | solution.py:17
  326.8 15.5 %fusion.2 = f32[8,128,128,8]{2,1,3,0:T(8,128)} fusion(f32[8,1024,128,8]{2,1,3,0:T(8,128)} %get-tuple-element.15, f32[128,8,8]{0,2,1:T(8,128)S(1)} %add.63, f32[128,8,8]{0,2,1:T(8,128)S(1)} %max.9, bf16[1024,8,128,1]{2,1,0,3:T(8,128)(2,1)S(1)} %bitcast.80), kind=kOutput, calls=%fused_computation.12 | convolution fusion | flops 2181038080 | bytes 39911424 | tf_op jit(solution)/shard_map/rcgqt,rtgd->rcgqd/dot_general | solution.py:20
  342.3 6.5 %fusion.5 = bf16[8,128,128,8]{2,1,3,0:T(8,128)(2,1)} fusion(f32[8,128,128,8]{2,1,3,0:T(8,128)} %fusion.2, f32[8,128,128,8]{2,1,3,0:T(8,128)} %get-tuple-element.17, f32[128,8,8]{0,2,1:T(8,128)S(1)} %add.63, f32[128,8,8]{0,2,1:T(8,128)S(1)} %max.9, pred[128,128]{0,1:T(8,128)(4,1)S(1)} %iota_compare_fusion, bf16[128,8,128,1]{2,1,0,3:T(8,128)(2,1)S(1)} %bitcast.85), kind=kOutput, calls=%fused_computation.17 | convolution fusion | flops 275775488 | bytes 10829824 | tf_op jit(solution)/shard_map/rcgqt,rtgd->rcgqd/dot_general | solution.py:21
  348.8 4.1 %copy.45 = bf16[1,128,64,128]{3,2,1,0:T(8,128)(2,1)} copy(bf16[1,128,64,128]{1,3,2,0:T(8,128)(2,1)} %bitcast.81) | data formatting | bytes 4194304
  (37 shorter events, 0.4 us)
Async XLA Ops:
  0.6 185.2 %copy-start = (bf16[1,128,64,128]{3,2,1,0:T(8,128)(2,1)S(1)}, bf16[1,128,64,128]{3,2,1,0:T(8,128)(2,1)}, u32[]{:S(2)}) copy-start(bf16[1,128,64,128]{3,2,1,0:T(8,128)(2,1)} %param.7) | copy-start | bytes 6291460
  0.6 4.1 %copy-start.9 = (s32[2]{0:T(128)S(1)}, s32[2]{0:T(128)}, u32[]{:S(2)}) copy-start(s32[2]{0:T(128)} %constant.76) | copy-start | bytes 28
  0.7 4.2 %copy-start.8 = (s32[2]{0:T(128)S(1)}, s32[2]{0:T(128)}, u32[]{:S(2)}) copy-start(s32[2]{0:T(128)} %constant.73) | copy-start | bytes 28
  0.7 3.7 %copy-start.7 = (s32[128,64]{0,1:T(8,128)S(1)}, s32[128,64]{0,1:T(8,128)}, u32[]{:S(2)}) copy-start(s32[128,64]{0,1:T(8,128)} %param.12) | copy-start | bytes 98308
  45.4 124.9 %all-to-all-start = ((bf16[128,2,16,8,128]{4,3,2,1,0:T(8,128)(2,1)}), bf16[128,2,16,8,128]{4,3,2,1,0:T(8,128)(2,1)}, u32[]{:S(2)}, u32[]{:S(2)}) async-start(bf16[128,2,16,8,128]{4,3,2,1,0:T(8,128)(2,1)} %bitcast.78), calls=%async_computation | async-start | bytes 16777216 | tf_op jit(solution)/shard_map/all_to_all | solution.py:42
  170.3 12.0 %copy-start.10 = (s32[1,8]{1,0:T(1,128)S(1)}, s32[1,8]{1,0:T(1,128)}, u32[]{:S(2)}) copy-start(s32[1,8]{1,0:T(1,128)} %param.13) | copy-start | bytes 100
  170.3 14.5 %copy-start.5 = (bf16[1,128,8,128]{3,2,1,0:T(8,128)(2,1)S(1)}, bf16[1,128,8,128]{3,2,1,0:T(8,128)(2,1)}, u32[]{:S(2)}) copy-start(bf16[1,128,8,128]{3,2,1,0:T(8,128)(2,1)} %param.8) | copy-start | bytes 786436
  170.3 120.4 %all-to-all-start.1 = ((bf16[128,2,16,8,128]{4,3,2,1,0:T(8,128)(2,1)}), bf16[128,2,16,8,128]{4,3,2,1,0:T(8,128)(2,1)}, u32[]{:S(2)}, u32[]{:S(2)}) async-start(bf16[128,2,16,8,128]{4,3,2,1,0:T(8,128)(2,1)} %bitcast.77), calls=%async_computation.1 | async-start | bytes 16777216 | tf_op jit(solution)/shard_map/all_to_all | solution.py:41
  185.6 9.7 %copy-start.2 = (bf16[32,16,8,128]{3,2,1,0:T(8,128)(2,1)}, bf16[32,16,8,128]{3,2,1,0:T(8,128)(2,1)S(1)}, u32[]{:S(2)}) copy-start(bf16[32,16,8,128]{3,2,1,0:T(8,128)(2,1)S(1)} %scatter_fusion) | copy-start | bytes 3145732
  296.2 15.7 %copy-start.3 = (f32[8,128,128,8]{2,1,3,0:T(8,128)S(1)}, f32[8,128,128,8]{2,1,3,0:T(8,128)}, u32[]{:S(2)}) copy-start(f32[8,128,128,8]{2,1,3,0:T(8,128)} %get-tuple-element.17) | copy-start | bytes 12582916
  313.0 13.7 %copy-start.4 = (bf16[64,16,8,128]{3,2,1,0:T(8,128)(2,1)S(1)}, bf16[64,16,8,128]{3,2,1,0:T(8,128)(2,1)}, u32[]{:S(2)}) copy-start(bf16[64,16,8,128]{3,2,1,0:T(8,128)(2,1)} %gather_fusion.1) | copy-start | bytes 6291460
  326.7 15.5 %copy-start.6 = (bf16[1,128,8,128]{3,2,1,0:T(8,128)(2,1)S(1)}, bf16[1,128,8,128]{3,2,1,0:T(8,128)(2,1)}, u32[]{:S(2)}) copy-start(bf16[1,128,8,128]{3,2,1,0:T(8,128)(2,1)} %param.9) | copy-start | bytes 786436
  342.3 10.7 %copy-start.1 = (bf16[1,128,64,128]{3,2,1,0:T(8,128)(2,1)S(1)}, bf16[1,128,64,128]{3,2,1,0:T(8,128)(2,1)}, u32[]{:S(2)}) copy-start(bf16[1,128,64,128]{3,2,1,0:T(8,128)(2,1)} %param.7) | copy-start | bytes 6291460
where the time goes:
time: 358 us; the launch traced here: 353 us
  waiting for transfers between devices  200 us (56%)
  local copies, waits for them, and re-layouts  71.3 us (20%)
  matrix products  41.7 us (12%)
  starting transfers between devices  23.4 us (7%)
  other arithmetic  15.7 us (4%)
    all_to_all x1, waiting for transfers between devices, local_step(): v_recv = lax.all_to_all(v_pool[send_ids], 'pool', 0, 0, tiled=True)  105 us
    all_to_all x1, waiting for transfers between devices, local_step(): k_recv = lax.all_to_all(k_pool[send_ids], 'pool', 0, 0, tiled=True)  95.4 us
    unnamed x28, local copies, waits for them, and re-layouts  38.5 us
    dot_general x1, matrix products, chunk_attention(): jnp.einsum('rcgqd,rtgd->rcgqt', q_grp, k_pref, preferred_element_type=jnp...  15.7 us
    dot_general x1, matrix products, chunk_attention(): jnp.einsum('rcgqt,rtgd->rcgqd', p_pref, v_pref, preferred_element_type=jn...  15.5 us
    reduce_sum x1, other arithmetic, chunk_attention(): jnp.sum(e_pref, axis=-1, keepdims=True)  13.7 us
    all_to_all x1, starting transfers between devices, local_step(): v_recv = lax.all_to_all(v_pool[send_ids], 'pool', 0, 0, tiled=True)  12 us
    all_to_all x1, starting transfers between devices, local_step(): k_recv = lax.all_to_all(k_pool[send_ids], 'pool', 0, 0, tiled=True)  11.4 us
  transfers between devices with their start and end apart: 2, of which 2 were waited for; matrix products, arithmetic and copies ran while one was open for 6% of the time, Pallas kernels for 0%

commit v1 on v0

v1 whole, which is shorter than its diff:
```python
import functools

import jax
import jax.numpy as jnp
from jax import lax
from jax.experimental import pallas as pl
from jax.experimental.pallas import tpu as pltpu
from jax.sharding import PartitionSpec as P

MESH = pl.DeviceIdType.MESH
PLANES = 4
PLANE = 32
Z_CAP = 10
PAIR_CAP = 2
N_CH = 4
LOG2E = 1.4426950408889634
OFFSETS = ((0, 1), (1, 0), (0, 3), (3, 0), (1, 1), (3, 3), (1, 3), (3, 1), (0, 2), (2, 0), (1, 2), (2, 1), (3, 2), (2, 3), (2, 2), (0, 0))
ORDER = tuple((dy, dx, dc) for dc in range(2) for dy, dx in OFFSETS if (dy, dx, dc) != (0, 0, 0))


def plane_peer(pos, dy, dx, dc):
    y, x, c = lax.rem(pos // 8, 4), lax.rem(pos // 2, 4), lax.rem(pos, 2)
    return (lax.rem(y + dy, 4) * 4 + lax.rem(x + dx, 4)) * 2 + lax.rem(c + dc, 2)


def exchange_kernel(zidx_ref, bidx_ref, pool_ref, recv_ref, *scratch):
    zsend, zrecv, bsend = scratch[:N_CH], scratch[N_CH:2 * N_CH], scratch[2 * N_CH:3 * N_CH]
    zs_sem, zr_sem, bs_sem, br_sem = scratch[3 * N_CH:]
    me = lax.axis_index('pool')
    my_z, my_pos = me // PLANE, lax.rem(me, PLANE)
    base = my_z * PLANE

    barrier = pltpu.get_barrier_semaphore()
    for dz in range(1, PLANES):
        pl.semaphore_signal(barrier, inc=1, device_id=(lax.rem(my_z + dz, PLANES) * PLANE + my_pos,), device_id_type=MESH)

    @pl.loop(1, PLANE)
    def _(i):
        pl.semaphore_signal(barrier, inc=1, device_id=(base + lax.rem(my_pos + i, PLANE),), device_id_type=MESH)

    for ch in range(N_CH):
        @pl.loop(0, Z_CAP)
        def _(s):
            block = pool_ref[zidx_ref[s], ch]
            zsend[ch][s] = block
            zrecv[ch][my_z * Z_CAP + s] = block

    pl.semaphore_wait(barrier, PLANES - 1 + PLANE - 1)

    def z_copy(ch, dz):
        there = lax.rem(my_z + dz, PLANES)
        return pltpu.make_async_remote_copy(
            src_ref=zsend[ch], dst_ref=zrecv[ch].at[pl.ds(my_z * Z_CAP, Z_CAP)], send_sem=zs_sem.at[ch, dz], recv_sem=zr_sem.at[ch, dz],
            device_id=(there * PLANE + my_pos,), device_id_type=MESH)

    def b_copy(ch, peer):
        return pltpu.make_async_remote_copy(
            src_ref=bsend[ch].at[peer], dst_ref=recv_ref.at[ch, my_pos], send_sem=bs_sem.at[ch, peer], recv_sem=br_sem.at[ch, my_pos],
            device_id=(base + peer,), device_id_type=MESH)

    def b_arrival(ch, peer):
        return pltpu.make_async_remote_copy(
            src_ref=bsend[ch].at[peer], dst_ref=recv_ref.at[ch, peer], send_sem=bs_sem.at[ch, peer], recv_sem=br_sem.at[ch, peer],
            device_id=(base + peer,), device_id_type=MESH)

    for ch in range(N_CH):
        for dz in (1, 3, 2):
            z_copy(ch, dz).start()
    for ch in range(N_CH):
        for dz in (1, 3, 2):
            z_copy(ch, dz).wait_recv()

        @pl.loop(0, PLANE)
        def _(p):
            for s in range(PAIR_CAP):
                bsend[ch][p, :, s * 16:(s + 1) * 16, :] = zrecv[ch][bidx_ref[p * PAIR_CAP + s]]

        recv_ref[ch, my_pos] = bsend[ch][my_pos]
        for dy, dx, dc in ORDER:
            b_copy(ch, plane_peer(my_pos, dy, dx, dc)).start()
    for ch in range(N_CH):
        @pl.loop(1, PLANE)
        def _(i):
            b_arrival(ch, lax.rem(my_pos + i, PLANE)).wait_recv()
    for ch in range(N_CH):
        for dz in (1, 3, 2):
            z_copy(ch, dz).wait_send()

        @pl.loop(1, PLANE)
        def _(i):
            b_arrival(ch, lax.rem(my_pos + i, PLANE)).wait_send()


def exchange(zidx, bidx, pool_t):
    block = pool_t.shape[2:]
    dtype = pool_t.dtype
    pair = (block[0], PAIR_CAP * block[1], block[2])
    return pl.pallas_call(
        exchange_kernel,
        out_shape=jax.ShapeDtypeStruct((N_CH, PLANE) + pair, dtype),
        in_specs=[pl.BlockSpec(memory_space=pltpu.SMEM), pl.BlockSpec(memory_space=pltpu.SMEM), pl.BlockSpec(memory_space=pltpu.VMEM)],
        out_specs=pl.BlockSpec(memory_space=pltpu.VMEM),
        scratch_shapes=[pltpu.VMEM((Z_CAP,) + block, dtype)] * N_CH + [pltpu.VMEM((PLANES * Z_CAP,) + block, dtype)] * N_CH
        + [pltpu.VMEM((PLANE,) + pair, dtype)] * N_CH
        + [pltpu.SemaphoreType.DMA((N_CH, PLANES)), pltpu.SemaphoreType.DMA((N_CH, PLANES)),
           pltpu.SemaphoreType.DMA((N_CH, PLANE)), pltpu.SemaphoreType.DMA((N_CH, PLANE))],
        compiler_params=pltpu.CompilerParams(collective_id=0, has_side_effects=True, vmem_limit_bytes=48 << 20),
        name='exchange',
    )(zidx, bidx, pool_t)


def attention_kernel(q_ref, kv_ref, new_ref, out_ref):
    chunk_len, head_dim = q_ref.shape[0], q_ref.shape[2]
    scale = head_dim ** -0.5 * LOG2E
    group = 8
    tile = 32

    def nt(a, b):
        return lax.dot_general(a, b, (((1,), (1,)), ((), ())), preferred_element_type=jnp.float32)

    for hh in range(2):
        k_pref = kv_ref[0, :, hh].reshape(-1, head_dim)
        v_pref = kv_ref[0, :, 2 + hh].reshape(-1, head_dim)
        k_new, v_new = new_ref[0, hh], new_ref[0, 2 + hh]

        @pl.loop(0, chunk_len // tile)
        def _(t):
            q = q_ref[pl.ds(t * tile, tile), hh * group:(hh + 1) * group, :]
            q = q.astype(jnp.float32).reshape(tile * group, head_dim).astype(jnp.bfloat16)
            s_pref = nt(q, k_pref)
            s_self = nt(q, k_new)
            token = t * tile + lax.broadcasted_iota(jnp.int32, s_self.shape, 0) // group
            s_self = jnp.where(token >= lax.broadcasted_iota(jnp.int32, s_self.shape, 1), s_self, -jnp.inf)
            top = jnp.maximum(jnp.max(s_pref, axis=1, keepdims=True), jnp.max(s_self, axis=1, keepdims=True))
            e_pref = jnp.exp2((s_pref - top) * scale)
            e_self = jnp.exp2((s_self - top) * scale)
            inv = 1.0 / (jnp.sum(e_pref, axis=1, keepdims=True) + jnp.sum(e_self, axis=1, keepdims=True))
            p_pref = (e_pref * inv).astype(jnp.bfloat16)
            p_self = (e_self * inv).astype(jnp.bfloat16)
            acc = jnp.dot(p_pref, v_pref, preferred_element_type=jnp.float32) + jnp.dot(p_self, v_new, preferred_element_type=jnp.float32)
            out_ref[pl.ds(t * tile, tile), hh * group:(hh + 1) * group, :] = acc.reshape(tile, group, head_dim).astype(jnp.bfloat16)


def attention(q, kv, new):
    chunk_len, q_heads, head_dim = q.shape
    wide = q_heads // N_CH
    return pl.pallas_call(
        attention_kernel,
        grid=(N_CH,),
        out_shape=jax.ShapeDtypeStruct(q.shape, q.dtype),
        in_specs=[pl.BlockSpec((chunk_len, wide, head_dim), lambda c: (0, c, 0)),
                  pl.BlockSpec((1,) + kv.shape[1:], lambda c: (c, 0, 0, 0, 0)),
                  pl.BlockSpec((1,) + new.shape[1:], lambda c: (c, 0, 0, 0))],
        out_specs=pl.BlockSpec((chunk_len, wide, head_dim), lambda c: (0, c, 0)),
        compiler_params=pltpu.CompilerParams(vmem_limit_bytes=48 << 20),
        name='attention',
    )(q, kv, new)


def by_chunk(k, v):
    n, t, h, d = k.shape
    both = jnp.stack([k, v], axis=1).reshape(n, 2, t, N_CH, h // N_CH, d)
    return both.transpose(0, 3, 1, 4, 2, 5).reshape(n, N_CH, 2 * h // N_CH, t, d)


def plan(block_table, me, per_dev):
    n_dev = block_table.shape[0]
    owner, local = block_table // per_dev, block_table % per_dev
    col, plane = owner % PLANE, owner // PLANE
    in_col = jnp.sum((col[:, :, None] == jnp.arange(PLANE)).astype(jnp.int32), axis=1)
    own_hot = (owner.reshape(-1)[:, None] == jnp.arange(n_dev)).astype(jnp.bfloat16)
    loc_hot = (local.reshape(-1)[:, None] == jnp.arange(per_dev)).astype(jnp.bfloat16)
    named = lax.dot_general(own_hot, loc_hot, (((0,), (0,)), ((), ())), preferred_element_type=jnp.float32) > 0
    fits = (jnp.max(in_col) <= PAIR_CAP) & (jnp.max(jnp.sum(named.astype(jnp.int32), axis=1)) <= Z_CAP)
    my_z, my_pos = me // PLANE, me % PLANE
    mine = lax.dynamic_slice_in_dim(named.reshape(PLANES, PLANE, per_dev), my_pos, 1, 1)[:, 0]
    below = jnp.arange(per_dev)[:, None] < jnp.arange(per_dev)[None, :]
    rank = jnp.sum((mine[:, :, None] & below[None]).astype(jnp.int32), axis=1)
    sent = lax.dynamic_slice_in_dim(mine, my_z, 1, 0)[0]
    sent_rank = lax.dynamic_slice_in_dim(rank, my_z, 1, 0)[0]
    hit = sent[None, :] & (sent_rank[None, :] == jnp.arange(Z_CAP)[:, None])
    zidx = jnp.sum(jnp.where(hit, jnp.arange(per_dev)[None, :], 0), axis=1)
    key = plane * per_dev + local
    rows = lambda a: lax.dynamic_slice_in_dim(a, my_z * PLANE, PLANE, 0)
    match, row_key = rows(col) == my_pos, rows(key)
    n_keys = PLANES * per_dev
    first = jnp.min(jnp.where(match, row_key, n_keys - 1), axis=1)
    last = jnp.max(jnp.where(match, row_key, 0), axis=1)
    pair_key = jnp.stack([first, last], axis=1).reshape(-1)
    slot = jnp.minimum(jnp.arange(PLANES)[:, None] * Z_CAP + rank, PLANES * Z_CAP - 1).reshape(-1)
    bidx = jnp.sum(jnp.where(pair_key[:, None] == jnp.arange(n_keys)[None, :], slot[None, :], 0), axis=1)
    return fits, zidx.astype(jnp.int32), bidx.astype(jnp.int32)


def solution(mesh):
    n_dev = mesh.shape['pool']

    def padded_exchange(k_pool, v_pool, block_table):
        per_dev = k_pool.shape[0]
        n_pref = block_table.shape[1]
        my_index = lax.axis_index('pool')
        pair_cap = 2
        owners = block_table // per_dev
        owned_here = (owners == my_index).astype(jnp.int32)
        send_slot = jnp.where(owned_here > 0, jnp.cumsum(owned_here, axis=1) - 1, pair_cap)
        dest_dev = jnp.broadcast_to(jnp.arange(n_dev)[:, None], send_slot.shape)
        send_ids = jnp.zeros((n_dev, pair_cap), jnp.int32).at[dest_dev, send_slot].set(block_table % per_dev, mode='drop')
        k_recv = lax.all_to_all(k_pool[send_ids], 'pool', 0, 0, tiled=True)
        v_recv = lax.all_to_all(v_pool[send_ids], 'pool', 0, 0, tiled=True)
        my_owners = lax.dynamic_slice_in_dim(owners, my_index, 1, 0).reshape(-1)
        from_owner = (my_owners[:, None] == jnp.arange(n_dev)[None, :]).astype(jnp.int32)
        slot_rank = jnp.sum(from_owner * (jnp.cumsum(from_owner, axis=0) - 1), axis=1)
        recv_idx = my_owners * pair_cap + slot_rank
        flat = (n_dev * pair_cap,) + k_pool.shape[1:]
        pairs = by_chunk(k_recv.reshape(flat)[recv_idx], v_recv.reshape(flat)[recv_idx])
        parts, t, d = pairs.shape[2:]
        pairs = pairs.reshape(n_pref // PAIR_CAP, PAIR_CAP, N_CH, parts, t, d).transpose(2, 0, 3, 1, 4, 5)
        return pairs.reshape(N_CH, n_pref // PAIR_CAP, parts, PAIR_CAP * t, d)

    def local_step(queries, k_new, v_new, k_pool, v_pool, block_table, write_ids):
        chunk_len = queries.shape[1]
        per_dev, block_len = k_pool.shape[0], k_pool.shape[1]
        me = lax.axis_index('pool')
        fits, zidx, bidx = plan(block_table, me, per_dev)
        kv = lax.cond(
            fits,
            lambda: exchange(zidx, bidx, by_chunk(k_pool, v_pool)),
            lambda: padded_exchange(k_pool, v_pool, block_table))
        new = by_chunk(k_new, v_new)[0]
        attn_out = attention(queries[0], kv, new)[None]
        new_shape = (chunk_len // block_len, block_len) + k_new.shape[2:]
        targets = write_ids.reshape(-1)
        k_pool_out = k_pool.at[targets].set(k_new.reshape(new_shape))
        v_pool_out = v_pool.at[targets].set(v_new.reshape(new_shape))
        return attn_out, k_pool_out, v_pool_out

    row_spec = P('pool')
    return jax.shard_map(local_step, mesh=mesh, in_specs=(row_spec, row_spec, row_spec, row_spec, row_spec, P(), row_spec), out_specs=(row_spec, row_spec, row_spec), check_vma=False)
```

time: 358 us -> 134 us (0.37); the launches traced: 353 us -> 134 us
  waiting for transfers between devices: 200 us -> 0 us
  Pallas kernels: 0 us -> 110 us
  local copies, waits for them, and re-layouts: 71.3 us -> 14.6 us
  matrix products: 41.7 us -> 1.31 us
  starting transfers between devices: 23.4 us -> 0 us
  other arithmetic: 15.7 us -> 5.18 us
    all_to_all x2 -> x0, waiting for transfers between devices: 200 us -> none  [the longest x1 105 us: local_step(): v_recv = lax.all_to_all(v_pool[send_ids], 'pool', 0, 0, tiled=True)]
    pallas_call x0 -> x2, Pallas kernels: none -> 110 us  [the longest x1 78.4 us: exchange(): pl.pallas_call(exchange_kernel, out_shape=jax.ShapeDtypeStruct((N_CH, PLA...]
    dot_general x4 -> x1, matrix products: 41.7 us -> 1.31 us  [plan(): lax.dot_general(own_hot, loc_hot, (((0,), (0,)), ((), ())), preferred_ele...]
    unnamed x28 -> x13, local copies, waits for them, and re-layouts: 38.5 us -> 4.64 us
    gather x4 -> x0, local copies, waits for them, and re-layouts: 29 us -> none  [the longest x1 9.6 us: local_step(): v_recv = lax.all_to_all(v_pool[send_ids], 'pool', 0, 0, tiled=True)]
    all_to_all x2 -> x0, starting transfers between devices: 23.4 us -> none  [the longest x1 12 us: local_step(): v_recv = lax.all_to_all(v_pool[send_ids], 'pool', 0, 0, tiled=True)]
    reduce_sum x3 -> x4, other arithmetic: 15 us -> 2.22 us  [the longest x1 1.03 us: plan(): zidx = jnp.sum(jnp.where(hit, jnp.arange(per_dev)[None, :], 0), axis=1)]
    another operation x0 -> x6, local copies, waits for them, and re-layouts: none -> 3.62 us  [the longest x4 2.83 us: by_chunk(): both = jnp.stack([k, v], axis=1).reshape(n, 2, t, N_CH, h // N_CH, d)]
  transfers between devices with their start and end apart: 2 -> 0, of which waited for: 2 -> 0; matrix products, arithmetic and copies ran while one was open for 6% -> 0% of each run, Pallas kernels for 0% -> 0%
where the time goes in v1:
time: 134 us
  Pallas kernels  110 us (82%)
  local copies, waits for them, and re-layouts  14.6 us (11%)
  other arithmetic  5.18 us (4%)
  between operations  2.1 us (2%)
    pallas_call x1, Pallas kernels, exchange(): pl.pallas_call(exchange_kernel, out_shape=jax.ShapeDtypeStruct((N_CH, PLA...  78.4 us
    pallas_call x1, Pallas kernels, attention(): pl.pallas_call(attention_kernel, grid=(N_CH,), out_shape=jax.ShapeDtypeSt...  31.7 us
    unnamed x13, local copies, waits for them, and re-layouts  4.64 us
    another operation x4, local copies, waits for them, and re-layouts, by_chunk(): both = jnp.stack([k, v], axis=1).reshape(n, 2, t, N_CH, h // N_CH, d)  2.83 us

profile of v1, /device:TPU:1, one launch (start us, length us, event | category | flops | bytes accessed | tf_op | source)
XLA Modules:
  0.0 133.6 jit_solution(1734467826618263841)
XLA Ops:
  0.6 2.3 %copy.97 = bf16[32,16,8,128]{3,2,1,0:T(8,128)(2,1)} copy(bf16[32,16,8,128]{3,2,1,0:T(8,128)(2,1)} %param.12) | data formatting | bytes 2097152
  3.0 1.2 copy.98
  4.3 0.1 select_reduce_fusion.4
  4.4 0.5 pad_add_fusion.1
  5.0 0.1 copy.78
  5.1 0.1 copy.77
  5.3 1.3 convert_reduce_fusion.2
  6.7 0.1 constant_dynamic-slice_fusion.1
  6.8 0.1 copy.90
  6.9 0.1 convert_reduce_fusion.1
  7.0 0.6 eq.125
  7.7 0.6 eq.119
  8.3 0.5 iota.49
  8.8 0.6 reduce_max.28
  10.1 0.2 convert_reduce_fusion
  10.2 0.6 reduce_max.27
  11.5 84.4 %conditional.1 = (bf16[4,32,4,32,128]{4,3,2,1,0:T(8,128)(2,1)}) conditional(s32[]{:T(128)} %convert_element_type.22, (s32[128,64]{0,1:T(8,128)S(1)}, bf16[32,16,8,128]{3,2,1,0:T(8,128)(2,1)}, bf16[32,16,8,128]{3,2,1,0:T(8,128)(2,1)S(1)}) %tuple.38, (bf16[32,16,8,128]{3,2,1,0:T(8,128)(2,1)}, bf16[32,16,8,128]{3,2,1,0:T(8,128)(2,1)S(1)}, ...), branch_computations={%region_9.14_spmd, %region_14.15_spmd} | conditional | flops 3582981 | bytes 126850736 | solution.py:225
  11.8 0.1 copy.82
  11.9 1.0 select_reduce_fusion.1.zidx_ref
  13.0 0.7 copy.83
  13.7 0.1 eq.131
  13.8 0.6 broadcast_multiply_fusion
  14.5 0.9 select_reduce_fusion.bidx_ref
  15.5 1.5 %copy.69 = bf16[32,1,16,4,2,128]{5,2,4,1,3,0:T(8,128)(2,1)S(1)} copy(bf16[32,1,16,4,2,128]{5,4,3,2,0,1:T(2,128)(2,1)} %bitcast.57) | data formatting | bytes 2097152 | tf_op jit(solution)/shard_map/cond/branch_1_fun/stack | solution.py:162
  17.0 0.3 copy.70
  17.3 0.2 pad_maximum_fusion
  17.5 78.4 %exchange.1 = bf16[4,32,4,32,128]{4,3,2,1,0:T(8,128)(2,1)} custom-call(s32[10]{0:T(128)S(1)} %select_reduce_fusion.1.zidx_ref, s32[64]{0:T(128)S(1)} %select_reduce_fusion.bidx_ref, bf16[32,4,4,16,128]{4,3,2,1,0:T(8,128)(2,1)S(1)} %bitcast.53), custom_call_target="tpu_custom_call" | custom-call | tf_op jit(solution)/shard_map/cond/branch_1_fun/exchange/pallas_call | solution.py:98
  96.0 1.0 copy.85
  97.1 31.7 %attention.1 = bf16[128,64,128]{2,1,0:T(8,128)(2,1)} custom-call(bf16[128,64,128]{2,1,0:T(8,128)(2,1)S(1)} %bitcast.54, bf16[4,32,4,32,128]{4,3,2,1,0:T(8,128)(2,1)} %get-tuple-element.213.kv_ref, bf16[4,4,128,128]{3,2,1,0:T(8,128)(2,1)S(1)} %bitcast.55), custom_call_target="tpu_custom_call" | custom-call | tf_op jit(solution)/shard_map/attention/pallas_call | solution.py:147
  128.8 2.2 %scatter_fusion = bf16[32,16,8,128]{3,2,1,0:T(8,128)(2,1)} fusion(bf16[32,16,8,128]{3,2,1,0:T(8,128)(2,1)} %copy.97, s32[8]{0:T(128)S(1)} %fusion.20, bf16[8,16,8,128]{3,2,1,0:T(8,128)(2,1)S(1)} %bitcast.66), kind=kCustom, calls=%fused_computation.5 | custom fusion | bytes 786464 | tf_op jit(solution)/shard_map/scatter | solution.py:233
  130.9 1.7 %scatter_fusion.1 = bf16[32,16,8,128]{3,2,1,0:T(8,128)(2,1)S(1)} fusion(bf16[32,16,8,128]{3,2,1,0:T(8,128)(2,1)S(1)} %copy.98, s32[8]{0:T(128)S(1)} %fusion.20, bf16[8,16,8,128]{3,2,1,0:T(8,128)(2,1)} %bitcast.68), kind=kCustom, calls=%fused_computation.6 | custom fusion | bytes 786464 | tf_op jit(solution)/shard_map/scatter | solution.py:234
  132.6 1.0 copy-done.1
  (24 shorter events, 0.6 us)
Async XLA Ops:
  0.6 3.5 %copy-start.4 = (s32[128,64]{0,1:T(8,128)S(1)}, s32[128,64]{0,1:T(8,128)}, u32[]{:S(2)}) copy-start(s32[128,64]{0,1:T(8,128)} %param.14) | copy-start | bytes 98308
  11.5 84.4 %copy-start.3 = (bf16[1,128,8,128]{3,2,1,0:T(8,128)(2,1)S(1)}, bf16[1,128,8,128]{3,2,1,0:T(8,128)(2,1)}, u32[]{:S(2)}) copy-start(bf16[1,128,8,128]{3,2,1,0:T(8,128)(2,1)} %param.10) | copy-start | bytes 786436
  11.5 85.5 %copy-start = (bf16[1,128,64,128]{3,2,1,0:T(8,128)(2,1)S(1)}, bf16[1,128,64,128]{3,2,1,0:T(8,128)(2,1)}, u32[]{:S(2)}) copy-start(bf16[1,128,64,128]{3,2,1,0:T(8,128)(2,1)} %param.9) | copy-start | bytes 6291460
  97.1 31.7 %copy-start.5 = (s32[1,8]{1,0:T(1,128)S(1)}, s32[1,8]{1,0:T(1,128)}, u32[]{:S(2)}) copy-start(s32[1,8]{1,0:T(1,128)} %param.15) | copy-start | bytes 100
  132.6 1.0 copy-start.1

commit v2 on v1

--- a/solution.py
+++ b/solution.py
@@ -1,5 +1,3 @@
-import functools
-
 import jax
 import jax.numpy as jnp
 from jax import lax
@@ -12,7 +10,9 @@
 PLANE = 32
 Z_CAP = 10
 PAIR_CAP = 2
-N_CH = 4
+N_CH = 8
+GROUP = 8
+TILE = 32
 LOG2E = 1.4426950408889634
 OFFSETS = ((0, 1), (1, 0), (0, 3), (3, 0), (1, 1), (3, 3), (1, 3), (3, 1), (0, 2), (2, 0), (1, 2), (2, 1), (3, 2), (2, 3), (2, 2), (0, 0))
 ORDER = tuple((dy, dx, dc) for dc in range(2) for dy, dx in OFFSETS if (dy, dx, dc) != (0, 0, 0))
@@ -23,12 +23,41 @@
     return (lax.rem(y + dy, 4) * 4 + lax.rem(x + dx, 4)) * 2 + lax.rem(c + dc, 2)
 
 
-def exchange_kernel(zidx_ref, bidx_ref, pool_ref, recv_ref, *scratch):
+def attend_head(q_ref, kv, new, out_ref, ch):
+    chunk_len, head_dim = q_ref.shape[0], q_ref.shape[2]
+    scale = head_dim ** -0.5 * LOG2E
+    heads = pl.ds(pl.multiple_of(ch * GROUP, GROUP), GROUP)
+    k_pref, v_pref = kv(0), kv(1)
+    k_new, v_new = new(0), new(1)
+
+    def nt(a, b):
+        return lax.dot_general(a, b, (((1,), (1,)), ((), ())), preferred_element_type=jnp.float32)
+
+    @pl.loop(0, chunk_len // TILE)
+    def _(t):
+        tokens = pl.ds(t * TILE, TILE)
+        q = q_ref[tokens, heads, :].astype(jnp.float32).reshape(TILE * GROUP, head_dim).astype(jnp.bfloat16)
+        s_pref = nt(q, k_pref)
+        s_self = nt(q, k_new)
+        token = t * TILE + lax.broadcasted_iota(jnp.int32, s_self.shape, 0) // GROUP
+        s_self = jnp.where(token >= lax.broadcasted_iota(jnp.int32, s_self.shape, 1), s_self, -jnp.inf)
+        top = jnp.maximum(jnp.max(s_pref, axis=1, keepdims=True), jnp.max(s_self, axis=1, keepdims=True))
+        e_pref = jnp.exp2((s_pref - top) * scale)
+        e_self = jnp.exp2((s_self - top) * scale)
+        inv = 1.0 / (jnp.sum(e_pref, axis=1, keepdims=True) + jnp.sum(e_self, axis=1, keepdims=True))
+        p_pref = (e_pref * inv).astype(jnp.bfloat16)
+        p_self = (e_self * inv).astype(jnp.bfloat16)
+        acc = jnp.dot(p_pref, v_pref, preferred_element_type=jnp.float32) + jnp.dot(p_self, v_new, preferred_element_type=jnp.float32)
+        out_ref[tokens, heads, :] = acc.reshape(TILE, GROUP, head_dim).astype(jnp.bfloat16)
+
+
+def exchange_kernel(zidx_ref, bidx_ref, q_ref, pool_ref, new_ref, out_ref, recv_ref, *scratch):
     zsend, zrecv, bsend = scratch[:N_CH], scratch[N_CH:2 * N_CH], scratch[2 * N_CH:3 * N_CH]
     zs_sem, zr_sem, bs_sem, br_sem = scratch[3 * N_CH:]
     me = lax.axis_index('pool')
     my_z, my_pos = me // PLANE, lax.rem(me, PLANE)
     base = my_z * PLANE
+    head_dim = q_ref.shape[2]
 
     barrier = pltpu.get_barrier_semaphore()
     for dz in range(1, PLANES):
@@ -60,7 +89,7 @@
 
     def b_arrival(ch, peer):
         return pltpu.make_async_remote_copy(
-            src_ref=bsend[ch].at[peer], dst_ref=recv_ref.at[ch, peer], send_sem=bs_sem.at[ch, peer], recv_sem=br_sem.at[ch, peer],
+            src_ref=bsend[0].at[peer], dst_ref=recv_ref.at[ch, peer], send_sem=bs_sem.at[ch, peer], recv_sem=br_sem.at[ch, peer],
             device_id=(base + peer,), device_id_type=MESH)
 
     for ch in range(N_CH):
@@ -78,10 +107,15 @@
         recv_ref[ch, my_pos] = bsend[ch][my_pos]
         for dy, dx, dc in ORDER:
             b_copy(ch, plane_peer(my_pos, dy, dx, dc)).start()
-    for ch in range(N_CH):
+
+    @pl.loop(0, N_CH)
+    def _(ch):
         @pl.loop(1, PLANE)
         def _(i):
             b_arrival(ch, lax.rem(my_pos + i, PLANE)).wait_recv()
+
+        attend_head(q_ref, lambda part: recv_ref[ch, :, part].reshape(-1, head_dim), lambda part: new_ref[ch, part], out_ref, ch)
+
     for ch in range(N_CH):
         for dz in (1, 3, 2):
             z_copy(ch, dz).wait_send()
@@ -91,67 +125,41 @@
             b_arrival(ch, lax.rem(my_pos + i, PLANE)).wait_send()
 
 
-def exchange(zidx, bidx, pool_t):
+def exchange_attention(zidx, bidx, q, pool_t, new):
     block = pool_t.shape[2:]
     dtype = pool_t.dtype
     pair = (block[0], PAIR_CAP * block[1], block[2])
+    vmem, smem = pl.BlockSpec(memory_space=pltpu.VMEM), pl.BlockSpec(memory_space=pltpu.SMEM)
     return pl.pallas_call(
         exchange_kernel,
-        out_shape=jax.ShapeDtypeStruct((N_CH, PLANE) + pair, dtype),
-        in_specs=[pl.BlockSpec(memory_space=pltpu.SMEM), pl.BlockSpec(memory_space=pltpu.SMEM), pl.BlockSpec(memory_space=pltpu.VMEM)],
-        out_specs=pl.BlockSpec(memory_space=pltpu.VMEM),
-        scratch_shapes=[pltpu.VMEM((Z_CAP,) + block, dtype)] * N_CH + [pltpu.VMEM((PLANES * Z_CAP,) + block, dtype)] * N_CH
+        out_shape=jax.ShapeDtypeStruct(q.shape, dtype),
+        in_specs=[smem, smem, vmem, vmem, vmem],
+        out_specs=vmem,
+        scratch_shapes=[pltpu.VMEM((N_CH, PLANE) + pair, dtype)]
+        + [pltpu.VMEM((Z_CAP,) + block, dtype)] * N_CH + [pltpu.VMEM((PLANES * Z_CAP,) + block, dtype)] * N_CH
         + [pltpu.VMEM((PLANE,) + pair, dtype)] * N_CH
         + [pltpu.SemaphoreType.DMA((N_CH, PLANES)), pltpu.SemaphoreType.DMA((N_CH, PLANES)),
            pltpu.SemaphoreType.DMA((N_CH, PLANE)), pltpu.SemaphoreType.DMA((N_CH, PLANE))],
-        compiler_params=pltpu.CompilerParams(collective_id=0, has_side_effects=True, vmem_limit_bytes=48 << 20),
-        name='exchange',
-    )(zidx, bidx, pool_t)
+        compiler_params=pltpu.CompilerParams(collective_id=0, has_side_effects=True, vmem_limit_bytes=56 << 20),
+        name='exchange_attention',
+    )(zidx, bidx, q, pool_t, new)
 
 
 def attention_kernel(q_ref, kv_ref, new_ref, out_ref):
-    chunk_len, head_dim = q_ref.shape[0], q_ref.shape[2]
-    scale = head_dim ** -0.5 * LOG2E
-    group = 8
-    tile = 32
-
-    def nt(a, b):
-        return lax.dot_general(a, b, (((1,), (1,)), ((), ())), preferred_element_type=jnp.float32)
-
-    for hh in range(2):
-        k_pref = kv_ref[0, :, hh].reshape(-1, head_dim)
-        v_pref = kv_ref[0, :, 2 + hh].reshape(-1, head_dim)
-        k_new, v_new = new_ref[0, hh], new_ref[0, 2 + hh]
-
-        @pl.loop(0, chunk_len // tile)
-        def _(t):
-            q = q_ref[pl.ds(t * tile, tile), hh * group:(hh + 1) * group, :]
-            q = q.astype(jnp.float32).reshape(tile * group, head_dim).astype(jnp.bfloat16)
-            s_pref = nt(q, k_pref)
-            s_self = nt(q, k_new)
-            token = t * tile + lax.broadcasted_iota(jnp.int32, s_self.shape, 0) // group
-            s_self = jnp.where(token >= lax.broadcasted_iota(jnp.int32, s_self.shape, 1), s_self, -jnp.inf)
-            top = jnp.maximum(jnp.max(s_pref, axis=1, keepdims=True), jnp.max(s_self, axis=1, keepdims=True))
-            e_pref = jnp.exp2((s_pref - top) * scale)
-            e_self = jnp.exp2((s_self - top) * scale)
-            inv = 1.0 / (jnp.sum(e_pref, axis=1, keepdims=True) + jnp.sum(e_self, axis=1, keepdims=True))
-            p_pref = (e_pref * inv).astype(jnp.bfloat16)
-            p_self = (e_self * inv).astype(jnp.bfloat16)
-            acc = jnp.dot(p_pref, v_pref, preferred_element_type=jnp.float32) + jnp.dot(p_self, v_new, preferred_element_type=jnp.float32)
-            out_ref[pl.ds(t * tile, tile), hh * group:(hh + 1) * group, :] = acc.reshape(tile, group, head_dim).astype(jnp.bfloat16)
+    head_dim = q_ref.shape[2]
+    attend_head(q_ref, lambda part: kv_ref[0, :, part].reshape(-1, head_dim), lambda part: new_ref[0, part], out_ref, 0)
 
 
 def attention(q, kv, new):
     chunk_len, q_heads, head_dim = q.shape
-    wide = q_heads // N_CH
     return pl.pallas_call(
         attention_kernel,
         grid=(N_CH,),
         out_shape=jax.ShapeDtypeStruct(q.shape, q.dtype),
-        in_specs=[pl.BlockSpec((chunk_len, wide, head_dim), lambda c: (0, c, 0)),
+        in_specs=[pl.BlockSpec((chunk_len, GROUP, head_dim), lambda c: (0, c, 0)),
                   pl.BlockSpec((1,) + kv.shape[1:], lambda c: (c, 0, 0, 0, 0)),
                   pl.BlockSpec((1,) + new.shape[1:], lambda c: (c, 0, 0, 0))],
-        out_specs=pl.BlockSpec((chunk_len, wide, head_dim), lambda c: (0, c, 0)),
+        out_specs=pl.BlockSpec((chunk_len, GROUP, head_dim), lambda c: (0, c, 0)),
         compiler_params=pltpu.CompilerParams(vmem_limit_bytes=48 << 20),
         name='attention',
     )(q, kv, new)
@@ -222,12 +230,11 @@
         per_dev, block_len = k_pool.shape[0], k_pool.shape[1]
         me = lax.axis_index('pool')
         fits, zidx, bidx = plan(block_table, me, per_dev)
-        kv = lax.cond(
+        new = by_chunk(k_new, v_new)[0]
+        attn_out = lax.cond(
             fits,
-            lambda: exchange(zidx, bidx, by_chunk(k_pool, v_pool)),
-            lambda: padded_exchange(k_pool, v_pool, block_table))
-        new = by_chunk(k_new, v_new)[0]
-        attn_out = attention(queries[0], kv, new)[None]
+            lambda: exchange_attention(zidx, bidx, queries[0], by_chunk(k_pool, v_pool), new),
+            lambda: attention(queries[0], padded_exchange(k_pool, v_pool, block_table), new))[None]
         new_shape = (chunk_len // block_len, block_len) + k_new.shape[2:]
         targets = write_ids.reshape(-1)
         k_pool_out = k_pool.at[targets].set(k_new.reshape(new_shape))

time: 134 us -> 102 us (0.76)
  Pallas kernels: 110 us -> 83.6 us
  local copies, waits for them, and re-layouts: 14.6 us -> 9.34 us
    pallas_call x2 -> x1, Pallas kernels: 110 us -> 83.6 us  [exchange_attention(): pl.pallas_call(exchange_kernel, out_shape=jax.ShapeDtypeStruct(q.shape, d...]
    another operation x4 -> x2, local copies, waits for them, and re-layouts: 2.83 us -> 0.7 us  [by_chunk(): both = jnp.stack([k, v], axis=1).reshape(n, 2, t, N_CH, h // N_CH, d)]
    reshape x0 -> x1, other arithmetic: none -> 1.51 us  [by_chunk(): both.transpose(0, 3, 1, 4, 2, 5).reshape(n, N_CH, 2 * h // N_CH, t, d)]
    unnamed x13 -> x16, local copies, waits for them, and re-layouts: 4.64 us -> 6.11 us
    scatter x1, local copies, waits for them, and re-layouts: 2.18 us -> 0.79 us  [local_step(): k_pool_out = k_pool.at[targets].set(k_new.reshape(new_shape))]
where the time goes in v2:
time: 102 us
  Pallas kernels  83.6 us (82%)
  local copies, waits for them, and re-layouts  9.34 us (9%)
  other arithmetic  4.78 us (5%)
  between operations  2.16 us (2%)
  matrix products  1.31 us (1%)
    pallas_call x1, Pallas kernels, exchange_attention(): pl.pallas_call(exchange_kernel, out_shape=jax.ShapeDtypeStruct(q.shape, d...  83.6 us
    unnamed x16, local copies, waits for them, and re-layouts  6.11 us

profile of v2, /device:TPU:1, one launch (start us, length us, event | category | flops | bytes accessed | tf_op | source)
XLA Modules:
  0.0 101.5 jit_solution(5534932106079201041)
XLA Ops:
  0.7 1.3 %copy.87 = bf16[32,16,8,128]{3,2,1,0:T(8,128)(2,1)S(1)} copy(bf16[32,16,8,128]{3,2,1,0:T(8,128)(2,1)} %param.12) | data formatting | bytes 2097152
  1.9 1.2 %copy.88 = bf16[32,16,8,128]{3,2,1,0:T(8,128)(2,1)S(1)} copy(bf16[32,16,8,128]{3,2,1,0:T(8,128)(2,1)} %param.13) | data formatting | bytes 2097152
  3.3 0.1 select_reduce_fusion.4
  3.4 0.1 copy.66
  3.5 0.1 eq.113
  3.6 0.1 copy.65
  3.7 0.1 eq.109
  3.8 1.3 %convert_reduce_fusion.2 = (s32[128]{0:T(128)S(1)}, pred[128,32]{0,1:T(8,128)(4,1)S(1)}) fusion(s32[8192]{0:T(1024)S(1)} %eq.113, s32[8192]{0:T(1024)S(1)} %eq.109), kind=kOutput, calls=%fused_computation.83 | convolution fusion | flops 68431744 | bytes 70144 | tf_op jit(solution)/shard_map/dot_general | solution.py:181
  5.1 0.1 reshape.153
  5.2 0.1 constant_dynamic-slice_fusion.1
  5.3 0.1 copy.75
  5.4 0.1 convert_reduce_fusion.1
  5.6 0.1 copy_bitcast_fusion.2
  5.7 0.1 maximum_bitcast_fusion.1
  5.8 0.6 reduce_max.28
  7.0 0.2 convert_reduce_fusion
  7.2 0.6 reduce_max.27
  8.5 87.9 %conditional.1 = (bf16[1,128,64,128]{3,2,1,0:T(8,128)(2,1)}) conditional(s32[]{:T(128)} %convert_element_type.22, (bf16[1,128,64,128]{3,2,1,0:T(8,128)(2,1)}, s32[128,64]{0,1:T(8,128)S(1)}, bf16[32,16,8,128]{3,2,1,0:T(8,128)(2,1)S(1)}, bf16[32,16,8,128]{3,2,1,0:T(8,128)(2,1)S(1)}, bf16[8,2,128,128]{3,2,1,0:T(8,128)(2,1)S(1)}) %tuple.44, ...), branch_computations={%region_9.14_spmd, %region_14.15_spmd} | conditional | flops 3582981 | bytes 118461624 | solution.py:234
  8.8 0.1 copy.72
  8.9 0.6 select_reduce_fusion.1.zidx_ref
  9.6 0.6 copy_bitcast_fusion
  10.2 1.5 %maximum_bitcast_fusion.pool_ref = bf16[32,8,2,16,128]{4,3,2,1,0:T(8,128)(2,1)} fusion(bf16[32,1,16,8,128]{4,2,1,3,0:T(8,128)(2,1)S(1)} %get-tuple-element.231, bf16[32,1,16,8,128]{4,2,1,3,0:T(8,128)(2,1)S(1)} %get-tuple-element.232), kind=kLoop, calls=%fused_computation.7 | loop fusion | flops 1048576 | bytes 4194304 | tf_op jit(solution)/shard_map/cond/branch_1_fun/reshape | solution.py:171
  11.7 0.1 copy.73
  11.8 0.1 eq.131
  11.9 0.1 add_minimum_fusion
  12.0 0.1 min.16
  12.0 0.7 select_reduce_fusion.bidx_ref
  12.8 83.6 %exchange_attention.1 = bf16[128,64,128]{2,1,0:T(8,128)(2,1)} custom-call(s32[10]{0:T(128)} %select_reduce_fusion.1.zidx_ref, s32[64]{0:T(128)} %select_reduce_fusion.bidx_ref, bf16[128,64,128]{2,1,0:T(8,128)(2,1)} %bitcast.72, bf16[32,8,2,16,128]{4,3,2,1,0:T(8,128)(2,1)} %maximum_bitcast_fusion.pool_ref, bf16[8,2,128,128]{3,2,1,0:T(8,128)(2,1)S(1)} %get-tuple-element.36.new_ref), custom_call_target="tpu_custom_call" | custom-call | tf_op jit(solution)/shard_map/cond/branch_1_fun/exchange_attention/pallas_call | solution.py:133
  96.4 0.8 scatter_fusion
  97.2 0.0 copy-start.1
  97.2 0.8 scatter_fusion.1
  98.0 3.5 %copy.89 = bf16[1,128,64,128]{3,2,1,0:T(8,128)(2,1)} copy(bf16[1,128,64,128]{3,2,1,0:T(8,128)(2,1)} %get-tuple-element.246) | data formatting | bytes 4194304
  (24 shorter events, 0.2 us)
Async XLA Ops:
  0.6 4.9 %copy-start.3 = (bf16[1,128,8,128]{3,2,1,0:T(8,128)(2,1)S(1)}, bf16[1,128,8,128]{3,2,1,0:T(8,128)(2,1)}, u32[]{:S(2)}) copy-start(bf16[1,128,8,128]{3,2,1,0:T(8,128)(2,1)} %param.10) | copy-start | bytes 786436
  0.6 4.9 %copy-start.4 = (bf16[1,128,8,128]{3,2,1,0:T(8,128)(2,1)S(1)}, bf16[1,128,8,128]{3,2,1,0:T(8,128)(2,1)}, u32[]{:S(2)}) copy-start(bf16[1,128,8,128]{3,2,1,0:T(8,128)(2,1)} %param.11) | copy-start | bytes 786436
  0.7 2.5 %copy-start.5 = (s32[128,64]{0,1:T(8,128)S(1)}, s32[128,64]{0,1:T(8,128)}, u32[]{:S(2)}) copy-start(s32[128,64]{0,1:T(8,128)} %param.14) | copy-start | bytes 98308
  8.5 87.9 %copy-start.6 = (s32[1,8]{1,0:T(1,128)S(1)}, s32[1,8]{1,0:T(1,128)}, u32[]{:S(2)}) copy-start(s32[1,8]{1,0:T(1,128)} %param.15) | copy-start | bytes 100
  97.2 4.3 %copy-start.1 = (bf16[32,16,8,128]{3,2,1,0:T(8,128)(2,1)}, bf16[32,16,8,128]{3,2,1,0:T(8,128)(2,1)S(1)}, u32[]{:S(2)}) copy-start(bf16[32,16,8,128]{3,2,1,0:T(8,128)(2,1)S(1)} %scatter_fusion) | copy-start | bytes 3145732
  98.0 3.5 %copy-start = (bf16[32,16,8,128]{3,2,1,0:T(8,128)(2,1)}, bf16[32,16,8,128]{3,2,1,0:T(8,128)(2,1)S(1)}, u32[]{:S(2)}) copy-start(bf16[32,16,8,128]{3,2,1,0:T(8,128)(2,1)S(1)} %scatter_fusion.1) | copy-start | bytes 3145732
